TPU v7x, 32 devices: a whole 2x2x4 slice. The times are simulated.
32 devices in a mesh: grp: 4 (over z), blk: 4 (over x, core), tp: 2 (over y).
Axes of the slice: x: 2, y: 2, z: 4, core: 2. Of those that a mesh axis runs over, the one named last changes fastest.
Arguments:
- queries: bfloat16 [512, 4096], P('grp', ('blk', 'tp')), may hold values from -110 to 110
- keys: bfloat16 [512, 4096], P('grp', ('blk', 'tp')), may hold values from -5 to 5
- values: bfloat16 [512, 4096], P('grp', ('blk', 'tp')), may hold values from -6 to 6
- cross_queries: bfloat16 [512, 4096], P('grp', ('blk', 'tp')), may hold values from -110 to 110
- history_keys: bfloat16 [768, 4096], P('grp', ('blk', 'tp')), may hold values from -5 to 5
- history_values: bfloat16 [768, 4096], P('grp', ('blk', 'tp')), may hold values from -6 to 6
- frame_ids: int32 [512], replicated, may hold values from 0 to 7, never falling along the last dimension, each value on 1 to 128 neighbouring positions
- masked: int32 [512], replicated, may hold values 0 or 1
- out_weight: bfloat16 [4096, 5120], P(('blk', 'tp')), may hold values from -0.09375 to 0.09375
- cotangent: bfloat16 [512, 5120], P('grp', ('blk', 'tp')), may hold values from -6 to 6
Outputs:
- layer_out: bfloat16 [512, 5120], P('grp', ('blk', 'tp'))
- query_grad: bfloat16 [512, 4096], P('grp', ('blk', 'tp'))
- key_grad: bfloat16 [512, 4096], P('grp', ('blk', 'tp'))
- value_grad: bfloat16 [512, 4096], P('grp', ('blk', 'tp'))
- cross_query_grad: bfloat16 [512, 4096], P('grp', ('blk', 'tp'))
- history_key_grad: bfloat16 [768, 4096], P('grp', ('blk', 'tp'))
- history_value_grad: bfloat16 [768, 4096], P('grp', ('blk', 'tp'))
- weight_grad: float32 [4096, 5120], P(('blk', 'tp'), 'grp')
Inputs may be any that keep to these rules, and one draw needn't show every extreme that they name: `frame_ids`: frame numbers never fall along the tokens; a frame holds 1 to 128 tokens.
All inputs are finite; a program needn't handle non-finite values.
Results may differ from a plain program's by a relative error of at most 0.017.
Values may be sent and summed in bfloat16 or wider, within the bound.
No kernel may reach another device: no remote copies, remote signals or barrier semaphores. Data moves between devices by JAX's collectives and lax.ppermute only.
A program may use at most 128 MiB of HBM per device.

v0:
```python
import jax
import jax.numpy as jnp
from jax import lax
from jax.sharding import PartitionSpec as P

HD = 128


def split_heads(matrix):
    return matrix.reshape(matrix.shape[0], matrix.shape[1] // HD, HD)


def merge_heads(tensor):
    return tensor.reshape(tensor.shape[0], tensor.shape[1] * tensor.shape[2])


def visible(query_frames, key_frames, key_masked, query_index, key_index):
    causal = key_frames[None, :] <= query_frames[:, None]
    open_key = (key_masked[None, :] == 0) | (key_index[None, :] == query_index[:, None])
    return causal & open_key


def scores_of(query_split, key_split, factor):
    return (
        jnp.einsum("qhd,khd->hqk", query_split, key_split, preferred_element_type=jnp.float32)
        * factor
    )


def softmax_parts(score):
    highest = jnp.max(score, axis=-1, keepdims=True)
    weights = jnp.exp(score - highest)
    summed = jnp.sum(weights, axis=-1, keepdims=True)
    return (weights / summed, highest[..., 0] + jnp.log(summed[..., 0]))


def key_side(dscore, prob_low, query_split, grad_split, factor):
    key_part = merge_heads(
        jnp.einsum("hqk,qhd->khd", dscore, query_split, preferred_element_type=jnp.float32) * factor
    )
    value_part = merge_heads(
        jnp.einsum("hqk,qhd->khd", prob_low, grad_split, preferred_element_type=jnp.float32)
    )
    return (key_part, value_part)


def on_device(
    queries,
    keys,
    values,
    cross_queries,
    history_keys,
    history_values,
    frame_ids,
    masked,
    out_weight,
    cotangent,
):
    row_count = queries.shape[0]
    factor = HD ** (-0.5)
    row_start = lax.axis_index("grp") * row_count
    query_index = row_start + jnp.arange(row_count, dtype=jnp.int32)
    every_key, every_value, past_keys, past_values = (
        lax.all_gather(keys, "grp", axis=0, tiled=True),
        lax.all_gather(values, "grp", axis=0, tiled=True),
        lax.all_gather(history_keys, "grp", axis=0, tiled=True),
        lax.all_gather(history_values, "grp", axis=0, tiled=True),
    )
    key_index = jnp.arange(every_key.shape[0], dtype=jnp.int32)
    query_frames = lax.dynamic_slice_in_dim(frame_ids, row_start, row_count)
    allowed = visible(query_frames, frame_ids, masked, query_index, key_index)
    query_split = split_heads(queries)
    cross_split = split_heads(cross_queries)
    key_split = split_heads(every_key)
    value_split = split_heads(every_value)
    memory_split = split_heads(past_keys)
    recall_split = split_heads(past_values)
    self_score = jnp.where(allowed[None], scores_of(query_split, key_split, factor), -jnp.inf)
    self_prob, self_log = softmax_parts(self_score)
    cross_prob, cross_log = softmax_parts(scores_of(cross_split, memory_split, factor))
    self_low = self_prob.astype(jnp.bfloat16)
    cross_low = cross_prob.astype(jnp.bfloat16)
    combined = jnp.einsum("hqk,khd->qhd", self_low, value_split, preferred_element_type=jnp.float32)
    combined = combined + jnp.einsum(
        "hqk,khd->qhd", cross_low, recall_split, preferred_element_type=jnp.float32
    )
    attended = merge_heads(combined).astype(jnp.bfloat16)
    head_terms = jnp.dot(attended, out_weight, preferred_element_type=jnp.float32)
    layer_out = lax.psum_scatter(head_terms, ("blk", "tp"), scatter_dimension=1, tiled=True).astype(
        jnp.bfloat16
    )
    arrived = lax.all_gather(cotangent, ("blk", "tp"), axis=1, tiled=True)
    grad_rows = lax.dot_general(
        arrived, out_weight, (((1,), (1,)), ((), ())), preferred_element_type=jnp.float32
    )
    product = lax.dot_general(
        attended, arrived, (((0,), (0,)), ((), ())), preferred_element_type=jnp.float32
    )
    grad_cols = product
    grad_rows, grad_cols = (grad_rows, grad_cols)
    weight_grad = lax.psum_scatter(
        grad_cols.astype(jnp.bfloat16), "grp", scatter_dimension=1, tiled=True
    ).astype(jnp.float32)
    grad_low = grad_rows.astype(jnp.bfloat16)
    grad_split = split_heads(grad_low)
    self_dprob = jnp.einsum(
        "qhd,khd->hqk", grad_split, value_split, preferred_element_type=jnp.float32
    )
    self_dot = jnp.sum(self_prob * self_dprob, axis=-1)
    self_dscore = (self_prob * (self_dprob - self_dot[..., None])).astype(jnp.bfloat16)
    cross_dprob = jnp.einsum(
        "qhd,khd->hqk", grad_split, recall_split, preferred_element_type=jnp.float32
    )
    cross_dot = jnp.sum(cross_prob * cross_dprob, axis=-1)
    cross_dscore = (cross_prob * (cross_dprob - cross_dot[..., None])).astype(jnp.bfloat16)
    query_grad = merge_heads(
        jnp.einsum("hqk,khd->qhd", self_dscore, key_split, preferred_element_type=jnp.float32)
        * factor
    ).astype(jnp.bfloat16)
    cross_grad = merge_heads(
        jnp.einsum("hqk,khd->qhd", cross_dscore, memory_split, preferred_element_type=jnp.float32)
        * factor
    ).astype(jnp.bfloat16)
    asked, asked_cross, asked_grad = (
        lax.all_gather(queries, "grp", axis=0, tiled=True),
        lax.all_gather(cross_queries, "grp", axis=0, tiled=True),
        lax.all_gather(grad_low, "grp", axis=0, tiled=True),
    )
    self_dots, cross_dots, self_logs, cross_logs = (
        lax.all_gather(self_dot, "grp", axis=1, tiled=True),
        lax.all_gather(cross_dot, "grp", axis=1, tiled=True),
        lax.all_gather(self_log, "grp", axis=1, tiled=True),
        lax.all_gather(cross_log, "grp", axis=1, tiled=True),
    )
    own_masked = lax.dynamic_slice_in_dim(masked, row_start, row_count)
    allowed_own = visible(frame_ids, query_frames, own_masked, key_index, query_index)
    asked_split = split_heads(asked)
    cross_every = split_heads(asked_cross)
    grad_every = split_heads(asked_grad)
    score_own = jnp.where(
        allowed_own[None], scores_of(asked_split, split_heads(keys), factor), -jnp.inf
    )
    prob_own = jnp.exp(score_own - self_logs[..., None])
    dprob_own = jnp.einsum(
        "qhd,khd->hqk", grad_every, split_heads(values), preferred_element_type=jnp.float32
    )
    dscore_own = (prob_own * (dprob_own - self_dots[..., None])).astype(jnp.bfloat16)
    key_part, value_part = key_side(
        dscore_own, prob_own.astype(jnp.bfloat16), asked_split, grad_every, factor
    )
    prob_past = jnp.exp(
        scores_of(cross_every, split_heads(history_keys), factor) - cross_logs[..., None]
    )
    dprob_past = jnp.einsum(
        "qhd,khd->hqk", grad_every, split_heads(history_values), preferred_element_type=jnp.float32
    )
    dscore_past = (prob_past * (dprob_past - cross_dots[..., None])).astype(jnp.bfloat16)
    memory_part, recall_part = key_side(
        dscore_past, prob_past.astype(jnp.bfloat16), cross_every, grad_every, factor
    )
    key_grad = key_part.astype(jnp.bfloat16)
    value_grad = value_part.astype(jnp.bfloat16)
    history_key_grad = memory_part.astype(jnp.bfloat16)
    history_value_grad = recall_part.astype(jnp.bfloat16)
    return (
        layer_out,
        query_grad,
        key_grad,
        value_grad,
        cross_grad,
        history_key_grad,
        history_value_grad,
        weight_grad,
    )


def solution(mesh):
    return jax.shard_map(
        on_device,
        mesh=mesh,
        in_specs=(
            P("grp", ("blk", "tp")),
            P("grp", ("blk", "tp")),
            P("grp", ("blk", "tp")),
            P("grp", ("blk", "tp")),
            P("grp", ("blk", "tp")),
            P("grp", ("blk", "tp")),
            P(),
            P(),
            P(("blk", "tp"), None),
            P("grp", ("blk", "tp")),
        ),
        out_specs=(
            P("grp", ("blk", "tp")),
            P("grp", ("blk", "tp")),
            P("grp", ("blk", "tp")),
            P("grp", ("blk", "tp")),
            P("grp", ("blk", "tp")),
            P("grp", ("blk", "tp")),
            P("grp", ("blk", "tp")),
            P(("blk", "tp"), "grp"),
        ),
        check_vma=False,
    )
```

profile of v0, /device:TPU:0, one launch (start us, length us, event | category | flops | bytes accessed | tf_op | source)
XLA Modules:
  0.0 245.7 jit_solution(7100060972051983405)
XLA Ops:
  7.2 0.0 all-gather.2.cloned.1.call-start
  7.2 0.7 all-gather.2.cloned.1.call-update
  7.9 0.0 reduce-scatter.3.cloned.1.call-start
  8.0 0.7 broadcast_compare_fusion
  8.7 1.0 copy.64
  9.7 16.7 %all_gather.36 = bf16[512,512]{0,1:T(8,128)(2,1)S(1)} all-gather(bf16[128,512]{0,1:T(8,128)(2,1)S(1)} %copy.64), channel_id=1, replica_groups=mesh['grp'=4,'blk'=4,'tp'=2] {'grp'}, dimensions={0}, use_global_device_ids=true | all-gather | bytes 655360 | tf_op jit(solution)/shard_map/all_gather | solution.py:64
  26.4 15.7 %all_gather.37 = bf16[512,512]{1,0:T(8,128)(2,1)S(1)} all-gather(bf16[128,512]{1,0:T(8,128)(2,1)} %param.12), channel_id=1, replica_groups=mesh['grp'=4,'blk'=4,'tp'=2] {'grp'}, dimensions={0}, use_global_device_ids=true | all-gather | bytes 655360 | tf_op jit(solution)/shard_map/all_gather | solution.py:65
  42.1 19.5 %all_gather.38 = bf16[768,512]{1,0:T(8,128)(2,1)S(1)} all-gather(bf16[192,512]{1,0:T(8,128)(2,1)S(1)} %copy-done.7), channel_id=1, replica_groups=mesh['grp'=4,'blk'=4,'tp'=2] {'grp'}, dimensions={0}, use_global_device_ids=true | all-gather | bytes 983040 | tf_op jit(solution)/shard_map/all_gather | solution.py:66
  61.6 15.7 %all_gather.39 = bf16[768,512]{1,0:T(8,128)(2,1)S(1)} all-gather(bf16[192,512]{1,0:T(8,128)(2,1)S(1)} %copy-done.9), channel_id=1, replica_groups=mesh['grp'=4,'blk'=4,'tp'=2] {'grp'}, dimensions={0}, use_global_device_ids=true | all-gather | bytes 983040 | tf_op jit(solution)/shard_map/all_gather | solution.py:67
  77.4 1.0 copy.67
  78.4 0.3 copy.68
  78.7 0.3 copy.71
  79.0 0.1 copy-done.18
  79.1 0.1 dynamic_slice.6
  79.2 0.1 fusion.43
  79.3 0.4 fusion.72
  79.7 0.3 fusion.20
  80.1 0.4 fusion.73
  80.5 0.4 fusion.1
  81.0 0.1 copy-done.14
  81.1 0.5 fusion.34
  81.6 0.1 copy-done
  81.7 0.6 fusion.17
  82.3 0.7 slice-done
  83.0 0.4 slice-done.1
  83.3 2.4 fusion.74
  85.7 0.0 reduce-scatter.3.cloned.1.call-update
  85.8 0.0 reduce-scatter.5.cloned.1.call-start
  85.8 0.0 all-gather.2.cloned.1.call-done
  85.8 5.1 %convolution_convert_fusion = bf16[512,5120]{1,0:T(8,128)(2,1)} fusion(bf16[128,512]{0,1:T(8,128)(2,1)S(1)} %bitcast.154, bf16[128,5120]{1,0:T(8,128)(2,1)} %all-gather.2.cloned.1.call-done), kind=kOutput, calls=%fused_computation | convolution fusion | flops 673710080 | bytes 6684672 | tf_op jit(solution)/shard_map/dot_general | solution.py:96
  91.0 0.1 copy.74
  91.1 0.1 copy.82
  91.3 11.9 %all_gather.42 = f32[4,512]{1,0:T(4,128)S(1)} all-gather(f32[4,128]{1,0:T(4,128)S(1)} %log_add_fusion.1), channel_id=1, replica_groups=mesh['grp'=4,'blk'=4,'tp'=2] {'grp'}, dimensions={1}, use_global_device_ids=true | all-gather | bytes 10240 | tf_op jit(solution)/shard_map/all_gather | solution.py:132
  103.2 11.9 %all_gather.46 = f32[4,512]{1,0:T(4,128)S(1)} all-gather(f32[4,128]{1,0:T(4,128)S(1)} %log_add_fusion), channel_id=1, replica_groups=mesh['grp'=4,'blk'=4,'tp'=2] {'grp'}, dimensions={1}, use_global_device_ids=true | all-gather | bytes 10240 | tf_op jit(solution)/shard_map/all_gather | solution.py:133
  115.1 0.8 dynamic-slice_compare_fusion
  115.9 14.9 %all_gather.45 = bf16[512,512]{0,1:T(8,128)(2,1)S(1)} all-gather(bf16[128,512]{0,1:T(8,128)(2,1)S(1)} %copy.82), channel_id=1, replica_groups=mesh['grp'=4,'blk'=4,'tp'=2] {'grp'}, dimensions={0}, use_global_device_ids=true | all-gather | bytes 655360 | tf_op jit(solution)/shard_map/all_gather | solution.py:126
  130.8 19.0 %all_gather.41 = bf16[512,512]{0,1:T(8,128)(2,1)S(1)} all-gather(bf16[128,512]{0,1:T(8,128)(2,1)S(1)} %copy.74), channel_id=1, replica_groups=mesh['grp'=4,'blk'=4,'tp'=2] {'grp'}, dimensions={0}, use_global_device_ids=true | all-gather | bytes 655360 | tf_op jit(solution)/shard_map/all_gather | solution.py:125
  149.8 0.1 fusion.45
  149.9 1.5 fusion.5
  151.4 0.4 subtract_exponential_fusion
  151.8 0.9 copy-done.2
  152.8 4.6 %convolution_convert_fusion.3 = bf16[128,512]{1,0:T(8,128)(2,1)S(1)} fusion(bf16[128,5120]{1,0:T(8,128)(2,1)S(1)} %copy-done.2, bf16[512,5120]{1,0:T(8,128)(2,1)} %param.18), kind=kOutput, calls=%fused_computation.31 | convolution fusion | flops 671154176 | bytes 6684672 | tf_op jit(solution)/shard_map/dot_general | solution.py:93
  157.4 0.4 multiply_reduce_fusion.1
  157.8 0.2 copy-done.12
  158.0 0.6 copy-done.19
  158.6 1.2 fusion.14
  159.8 1.7 copy.91
  161.5 24.1 %all_gather.43 = bf16[512,512]{1,0:T(8,128)(2,1)S(1)} all-gather(bf16[128,512]{1,0:T(8,128)(2,1)} %copy-done.12), channel_id=1, replica_groups=mesh['grp'=4,'blk'=4,'tp'=2] {'grp'}, dimensions={0}, use_global_device_ids=true | all-gather | bytes 655360 | tf_op jit(solution)/shard_map/all_gather | solution.py:127
  185.6 2.2 convolution_convert_fusion.2
  187.8 1.7 copy.93
  189.5 15.7 %all_gather.44 = f32[4,512]{1,0:T(4,128)S(1)} all-gather(f32[4,128]{1,0:T(4,128)} %copy-done.19), channel_id=1, replica_groups=mesh['grp'=4,'blk'=4,'tp'=2] {'grp'}, dimensions={1}, use_global_device_ids=true | all-gather | bytes 10240 | tf_op jit(solution)/shard_map/all_gather | solution.py:130
  205.2 2.6 %fusion.16 = bf16[4,128,128]{1,2,0:T(8,128)(2,1)} fusion(bf16[512,4,128]{0,2,1:T(8,128)(2,1)} %bitcast.152, f32[4,512,128]{2,1,0:T(8,128)} %fusion.5, f32[4,512]{1,0:T(4,128)S(1)} %all_gather.44, bf16[512,512]{1,0:T(8,128)(2,1)S(1)} %all_gather.43, bf16[128,512]{1,0:T(8,128)(2,1)S(1)} %copy-done.11), kind=kOutput, calls=%fused_computation.32 | convolution fusion | flops 135135232 | bytes 2367488 | tf_op jit(solution)/shard_map/hqk,qhd->khd/dot_general | solution.py:39
  207.8 1.7 copy.92
  209.5 2.4 multiply_reduce_fusion
  211.9 0.7 fusion.18
  212.6 0.8 copy.94
  213.4 0.4 fusion.15
  213.8 0.7 copy.174
  214.5 14.2 %all_gather.47 = f32[4,512]{1,0:T(4,128)S(1)} all-gather(f32[4,128]{1,0:T(4,128)S(1)} %get-tuple-element.38), channel_id=1, replica_groups=mesh['grp'=4,'blk'=4,'tp'=2] {'grp'}, dimensions={1}, use_global_device_ids=true | all-gather | bytes 10240 | tf_op jit(solution)/shard_map/all_gather | solution.py:131
  228.7 0.6 fusion.13
  229.3 0.7 copy.175
  230.0 1.7 convert_element_type.104
  231.6 4.6 %reduce-scatter.5.cloned.1.call-done = bf16[512,1280]{1,0:T(8,128)(2,1)} async-done(((bf16[512,5120]{1,0:T(8,128)(2,1)}), bf16[512,1280]{1,0:T(8,128)(2,1)}) %reduce-scatter.5.cloned.1.call-update) | async-done | bytes 1310736 | tf_op jit(solution)/shard_map/reduce_scatter | solution.py:101
  236.2 3.0 %convert_element_type.131 = f32[512,1280]{1,0:T(8,128)} convert(bf16[512,1280]{1,0:T(8,128)(2,1)} %reduce-scatter.5.cloned.1.call-done) | non-fusion elementwise | flops 655360 | bytes 3932160 | tf_op jit(solution)/shard_map/convert_element_type | solution.py:103
  (42 shorter events, 0.1 us)
Async XLA Ops:
  7.2 34.9 %copy-start.7 = (bf16[192,512]{1,0:T(8,128)(2,1)S(1)}, bf16[192,512]{1,0:T(8,128)(2,1)}, u32[]{:S(2)}) copy-start(bf16[192,512]{1,0:T(8,128)(2,1)} %param.14) | copy-start | bytes 589828
  7.2 54.5 %copy-start.9 = (bf16[192,512]{1,0:T(8,128)(2,1)S(1)}, bf16[192,512]{1,0:T(8,128)(2,1)}, u32[]{:S(2)}) copy-start(bf16[192,512]{1,0:T(8,128)(2,1)} %param.15) | copy-start | bytes 589828
  7.2 78.6 %all-gather.2.cloned.1.call-start = ((), (), s32[]{:S(2)}) async-start(), calls=%async_computation.3 | async-start | bytes 1474560 | tf_op jit(solution)/shard_map/all_gather | solution.py:92
  7.9 222.0 %reduce-scatter.3.cloned.1.call-start = ((), (), s32[]{:S(2)}) async-start(), calls=%async_computation.2 | async-start | bytes 2949120 | tf_op jit(solution)/shard_map/reduce_scatter | solution.py:89
  78.4 0.7 copy-start.18
  78.4 0.9 copy-start.16
  79.0 2.6 %copy-start.6 = (bf16[768,512]{0,1:T(8,128)(2,1)}, bf16[768,512]{0,1:T(8,128)(2,1)S(1)}, u32[]{:S(2)}) copy-start(bf16[768,512]{0,1:T(8,128)(2,1)S(1)} %copy.71) | copy-start | bytes 2359300
  79.0 1.1 copy-start.13
  79.7 1.3 copy-start.3
  80.0 1.1 copy-start.14
  80.0 2.9 %slice-start = ((s8[5242880]{0:T(1024)(128)(4,1)}), s8[4194304]{0:T(1024)(128)(4,1)S(1)}, s32[]{:S(2)}) async-start(s8[5242880]{0:T(1024)(128)(4,1)} %bitcast.143), calls=%async_computation.5 | async-start | bytes 8388608
  80.5 1.2 copy-start
  81.1 2.2 slice-start.1
  85.8 150.4 %reduce-scatter.5.cloned.1.call-start = ((), (), s32[]{:S(2)}) async-start(), calls=%async_computation.4 | async-start | bytes 6553600 | tf_op jit(solution)/shard_map/reduce_scatter | solution.py:101
  91.0 58.9 %copy-start.17 = (bf16[128,512]{1,0:T(8,128)(2,1)S(1)}, bf16[128,512]{1,0:T(8,128)(2,1)}, u32[]{:S(2)}) copy-start(bf16[128,512]{1,0:T(8,128)(2,1)} %param.11) | copy-start | bytes 393220
  115.9 35.5 %copy-start.8 = (bf16[192,512]{1,0:T(8,128)(2,1)S(1)}, bf16[192,512]{1,0:T(8,128)(2,1)}, u32[]{:S(2)}) copy-start(bf16[192,512]{1,0:T(8,128)(2,1)} %param.14) | copy-start | bytes 589828
  149.8 1.7 copy-start.5
  151.4 1.3 copy-start.2
  152.7 4.6 %copy-start.4 = (f32[4,128,512]{2,1,0:T(8,128)S(1)}, f32[4,128,512]{2,1,0:T(8,128)}, u32[]{:S(2)}) copy-start(f32[4,128,512]{2,1,0:T(8,128)} %copy-done.3) | copy-start | bytes 3145732
  152.7 4.6 %copy-start.15 = (bf16[512,512]{0,1:T(8,128)(2,1)S(1)}, bf16[512,512]{0,1:T(8,128)(2,1)}, u32[]{:S(2)}) copy-start(bf16[512,512]{0,1:T(8,128)(2,1)} %copy.67) | copy-start | bytes 1572868
  157.4 0.7 copy-start.12
  158.0 0.6 copy-start.19
  159.8 45.4 %copy-start.11 = (bf16[128,512]{1,0:T(8,128)(2,1)S(1)}, bf16[128,512]{1,0:T(8,128)(2,1)}, u32[]{:S(2)}) copy-start(bf16[128,512]{1,0:T(8,128)(2,1)} %param.12) | copy-start | bytes 393220
  209.5 2.4 copy-start.1
  212.6 16.1 %copy-start.10 = (bf16[192,512]{1,0:T(8,128)(2,1)S(1)}, bf16[192,512]{1,0:T(8,128)(2,1)}, u32[]{:S(2)}) copy-start(bf16[192,512]{1,0:T(8,128)(2,1)} %param.15) | copy-start | bytes 589828
Sparse Core Ops, SparseCore 0:
  9.9 27.1 all-gather.1
  85.9 44.0 reduce-scatter.2
  132.3 103.8 reduce-scatter.4
where the time goes:
time: 246 us
  blocking collectives  179 us (73%)
  matrix products  26.4 us (11%)
  between operations  14 us (6%)
  local copies, waits for them, and re-layouts  13.4 us (5%)
  other arithmetic  7.16 us (3%)
  waiting for transfers between devices  5.31 us (2%)
    all_gather x1, blocking collectives, on_device(): lax.all_gather(grad_low, 'grp', axis=0, tiled=True)  24.1 us
    all_gather x1, blocking collectives, on_device(): lax.all_gather(history_keys, 'grp', axis=0, tiled=True)  19.5 us
    all_gather x1, blocking collectives, on_device(): lax.all_gather(queries, 'grp', axis=0, tiled=True)  19 us
    all_gather x1, blocking collectives, on_device(): lax.all_gather(keys, 'grp', axis=0, tiled=True)  16.7 us
    all_gather x1, blocking collectives, on_device(): lax.all_gather(history_values, 'grp', axis=0, tiled=True)  15.7 us
    all_gather x1, blocking collectives, on_device(): lax.all_gather(self_dot, 'grp', axis=1, tiled=True)  15.7 us
    all_gather x1, blocking collectives, on_device(): lax.all_gather(values, 'grp', axis=0, tiled=True)  15.7 us
    all_gather x1, blocking collectives, on_device(): lax.all_gather(cross_queries, 'grp', axis=0, tiled=True)  14.9 us
  transfers between devices with their start and end apart: 3, of which 1 were waited for; matrix products, arithmetic and copies ran while one was open for 17% of the time, Pallas kernels for 0%

commit v1 on v0

--- a/solution.py
+++ b/solution.py
@@ -44,7 +44,7 @@
     return (key_part, value_part)
 
 
-def on_device(
+def on_device_tokens(
     queries,
     keys,
     values,
@@ -174,6 +174,212 @@
     )
 
 
+def rotated(slots, me):
+    n = len(slots)
+    twice = jnp.stack(slots[::-1] + slots[::-1])
+    return lax.dynamic_slice_in_dim(twice, n - 1 - me, n, axis=0)
+
+
+def shifted(piece, axis, shift, size):
+    return lax.ppermute(piece, axis, [(i, (i + shift) % size) for i in range(size)])
+
+
+def flipped(piece, axis, bit, size):
+    return lax.ppermute(piece, axis, [(i, i ^ bit) for i in range(size)])
+
+
+def ordered(flag, own, other):
+    return jnp.where(flag == 0, jnp.concatenate([own, other]), jnp.concatenate([other, own]))
+
+
+def plane_gather(piece, blk_size, tp_size):
+    blk, tp = lax.axis_index("blk"), lax.axis_index("tp")
+    steps = [(bit, shift) for bit in range(0, blk_size, 2) for shift in range(tp_size) if bit or shift]
+    got = {(0, 0): piece}
+    for bit, shift in steps:
+        pairs = []
+        for b in range(blk_size):
+            for t in range(tp_size):
+                pairs.append((b * tp_size + t, (b ^ bit) * tp_size + (t + shift) % tp_size))
+        got[(bit, shift)] = lax.ppermute(piece, ("blk", "tp"), pairs)
+    rows = [
+        rotated([got[(bit, shift)] for shift in range(tp_size)], tp) for bit in range(0, blk_size, 2)
+    ]
+    level = 2
+    while level < blk_size:
+        flag = (blk // level) % 2
+        rows = [
+            ordered(flag, rows[2 * i], rows[2 * i + 1]) for i in range(len(rows) // 2)
+        ]
+        level *= 2
+    half = rows[0].reshape((blk_size // 2, tp_size) + piece.shape)
+    other = flipped(half, "blk", 1, blk_size)
+    flag = blk % 2
+    both = jnp.where(
+        flag == 0, jnp.stack([half, other], axis=1), jnp.stack([other, half], axis=1)
+    )
+    return both.reshape((blk_size * tp_size,) + piece.shape)
+
+
+def on_device_heads(
+    grp, blk_size, tp_size, queries, keys, values, cross_queries, history_keys, history_values,
+    frame_ids, masked, out_weight, cotangent,
+):
+    bf16, f32 = jnp.bfloat16, jnp.float32
+    factor = HD ** (-0.5)
+    me = lax.axis_index("grp")
+    plane = lax.axis_index("blk") * tp_size + lax.axis_index("tp")
+    plane_size = blk_size * tp_size
+    row_count, width = queries.shape
+    past_count = history_keys.shape[0]
+    own_width = width // grp
+    heads = own_width // HD
+    sources = [queries, keys, values, cross_queries, history_keys, history_values]
+
+    def columns(array, rank):
+        return lax.dynamic_slice_in_dim(array, rank * own_width, own_width, 1)
+
+    def outgoing(shift):
+        rank = (me + shift) % grp
+        return jnp.concatenate([columns(array, rank) for array in sources])
+
+    came = [outgoing(0)] + [shifted(outgoing(s), "grp", s, grp) for s in range(1, grp)]
+    lengths = [row_count] * 4 + [past_count] * 2
+    starts = [sum(lengths[:i]) for i in range(6)]
+
+    arrived = plane_gather(cotangent, blk_size, tp_size)
+    cot_rows = jnp.moveaxis(arrived, 0, 1).reshape(row_count, -1)
+    grad_rows = lax.dot_general(
+        cot_rows, out_weight, (((1,), (1,)), ((), ())), preferred_element_type=f32
+    ).astype(bf16)
+    cot_width = cot_rows.shape[1] // grp
+    part_rows = row_count // plane_size
+    cot_part = lax.dynamic_slice_in_dim(cot_rows, plane * part_rows, part_rows, 0)
+
+    def grad_out(shift):
+        rank = (me + shift) % grp
+        piece = lax.dynamic_slice_in_dim(cot_part, rank * cot_width, cot_width, 1)
+        piece = piece.reshape(part_rows, cot_width // own_width, own_width).swapaxes(0, 1)
+        return jnp.concatenate([columns(grad_rows, rank), piece.reshape(-1, own_width)])
+
+    grads = [grad_out(0)] + [shifted(grad_out(s), "grp", s, grp) for s in range(1, grp)]
+    grad_head = jnp.concatenate([piece[:row_count] for piece in grads])
+    cot_mine = rotated([piece[row_count:] for piece in grads], me)
+    cot_mine = cot_mine.reshape(grp, cot_width // own_width, part_rows, own_width)
+    cot_mine = cot_mine.swapaxes(1, 2).reshape(grp, part_rows, cot_width)
+    cot_all = plane_gather(cot_mine.reshape(grp * part_rows, cot_width), blk_size, tp_size)
+    cot_all = cot_all.reshape(plane_size, grp, part_rows, cot_width).swapaxes(0, 1)
+    cot_all = cot_all.reshape(grp * row_count, cot_width)
+
+    def part(index):
+        return split_heads(
+            jnp.concatenate([piece[starts[index] : starts[index] + lengths[index]] for piece in came])
+        )
+
+    q, k, v, cq, hk, hv = [part(index) for index in range(6)]
+    slot_rank = (me - jnp.arange(grp, dtype=jnp.int32)) % grp
+    token = (slot_rank[:, None] * row_count + jnp.arange(row_count, dtype=jnp.int32)).reshape(-1)
+
+    def by_slot(vector):
+        parts = vector.reshape(grp, row_count)
+        return jnp.concatenate(
+            [lax.dynamic_index_in_dim(parts, (me - s) % grp, 0, keepdims=False) for s in range(grp)]
+        )
+
+    frames, hidden = by_slot(frame_ids), by_slot(masked)
+    allowed = visible(frames, frames, hidden, token, token)
+
+    def forward(query, key, limit):
+        score = scores_of(query, key, factor)
+        if limit is not None:
+            score = jnp.where(limit[None], score, -jnp.inf)
+        highest = jnp.max(score, axis=-1, keepdims=True)
+        weights = jnp.exp(score - highest)
+        return weights / jnp.sum(weights, axis=-1, keepdims=True)
+
+    self_prob = forward(q, k, allowed)
+    cross_prob = forward(cq, hk, None)
+    self_low, cross_low = self_prob.astype(bf16), cross_prob.astype(bf16)
+    combined = jnp.einsum("hqk,khd->qhd", self_low, v, preferred_element_type=f32)
+    combined = combined + jnp.einsum("hqk,khd->qhd", cross_low, hv, preferred_element_type=f32)
+    attended = merge_heads(combined).astype(bf16).reshape(grp, row_count, own_width)
+    attended = rotated([attended[s] for s in range(grp)], me).reshape(grp * row_count, own_width)
+
+    spread = [attended] + [shifted(attended, "grp", s, grp) for s in range(1, grp)]
+    att_heads = rotated(spread, me)
+    att_own = lax.dynamic_slice_in_dim(att_heads, me * row_count, row_count, 1)
+    att_own = att_own.swapaxes(0, 1).reshape(row_count, width)
+
+    gs = split_heads(grad_head)
+
+    def backward(prob, low, query, key, value):
+        dprob = jnp.einsum("qhd,khd->hqk", gs, value, preferred_element_type=f32)
+        dot = jnp.sum(prob * dprob, axis=-1, keepdims=True)
+        dscore = (prob * (dprob - dot)).astype(bf16)
+        dq = jnp.einsum("hqk,khd->qhd", dscore, key, preferred_element_type=f32) * factor
+        dk, dv = key_side(dscore, low, query, gs, factor)
+        return merge_heads(dq).astype(bf16), dk.astype(bf16), dv.astype(bf16)
+
+    dq, dk, dv = backward(self_prob, self_low, q, k, v)
+    dcq, dhk, dhv = backward(cross_prob, cross_low, cq, hk, hv)
+    results = [dq, dk, dv, dcq, dhk, dhv]
+
+    def returned(slot):
+        return jnp.concatenate(
+            [array[slot * size : (slot + 1) * size] for array, size in zip(results, lengths)]
+        )
+
+    back = [returned(0)] + [shifted(returned(s), "grp", -s, grp) for s in range(1, grp)]
+    twice = jnp.stack(back + back)
+    back = lax.dynamic_slice_in_dim(twice, (grp - me) % grp, grp, axis=0)
+
+    def restored(index):
+        piece = back[:, starts[index] : starts[index] + lengths[index]]
+        return piece.swapaxes(0, 1).reshape(lengths[index], width)
+
+    query_grad, key_grad, value_grad, cross_grad, hk_grad, hv_grad = [
+        restored(index) for index in range(6)
+    ]
+
+    weight_grad = jnp.einsum("gtf,tc->gfc", att_heads, cot_all, preferred_element_type=f32)
+    weight_grad = weight_grad.reshape(width, cot_width)
+
+    terms = jnp.dot(att_own, out_weight, preferred_element_type=f32).astype(bf16)
+    blocks = terms.reshape(row_count, blk_size // 2, 2, tp_size, -1).transpose(2, 1, 3, 0, 4)
+    low_bit = lax.axis_index("blk") % 2
+    mine = lax.dynamic_index_in_dim(blocks, low_bit, 0, keepdims=False)
+    theirs = lax.dynamic_index_in_dim(blocks, 1 - low_bit, 0, keepdims=False)
+    chip = mine.astype(f32) + flipped(theirs, "blk", 1, blk_size).astype(f32)
+    high, tp = lax.axis_index("blk") // 2, lax.axis_index("tp")
+    total = None
+    for bit in range(0, blk_size, 2):
+        for shift in range(tp_size):
+            piece = lax.dynamic_index_in_dim(chip, high ^ (bit // 2), 0, keepdims=False)
+            piece = lax.dynamic_index_in_dim(piece, (tp + shift) % tp_size, 0, keepdims=False)
+            if bit or shift:
+                pairs = []
+                for b in range(blk_size):
+                    for t in range(tp_size):
+                        pairs.append((b * tp_size + t, (b ^ bit) * tp_size + (t + shift) % tp_size))
+                piece = lax.ppermute(piece.astype(bf16), ("blk", "tp"), pairs).astype(f32)
+            total = piece if total is None else total + piece
+    layer_out = total.astype(bf16)
+    return (
+        layer_out, query_grad, key_grad, value_grad, cross_grad, hk_grad, hv_grad, weight_grad,
+    )
+
+
+def on_device(*operands):
+    grp, blk_size, tp_size = lax.axis_size("grp"), lax.axis_size("blk"), lax.axis_size("tp")
+    row_count, width = operands[0].shape
+    even = width % (grp * HD) == 0 and row_count % (16 * blk_size * tp_size) == 0
+    pairs = blk_size % 2 == 0 and blk_size & (blk_size - 1) == 0
+    fits = operands[8].shape[1] % (grp * (width // grp)) == 0
+    if even and pairs and fits:
+        return on_device_heads(grp, blk_size, tp_size, *operands)
+    return on_device_tokens(*operands)
+
+
 def solution(mesh):
     return jax.shard_map(
         on_device,

time: 246 us -> 131 us (0.53)
  blocking collectives: 179 us -> 0 us
  starting transfers between devices: 0.12 us -> 34.3 us
  local copies, waits for them, and re-layouts: 13.4 us -> 38.1 us
  waiting for transfers between devices: 5.31 us -> 29.3 us
  between operations: 14 us -> 1.87 us
  matrix products: 26.4 us -> 17.3 us
    all_gather x11 -> x0, blocking collectives: 179 us -> none  [the longest x1 24.1 us: on_device(): lax.all_gather(grad_low, 'grp', axis=0, tiled=True)]
    ppermute x0 -> x24, starting transfers between devices: none -> 34.3 us  [the longest x12 22 us: shifted(): lax.ppermute(piece, axis, [(i, (i + shift) % size) for i in range(size)])]
    ppermute x0 -> x24, waiting for transfers between devices: none -> 29.3 us  [the longest x12 27.8 us: shifted(): lax.ppermute(piece, axis, [(i, (i + shift) % size) for i in range(size)])]
    dynamic_slice x1 -> x12, local copies, waits for them, and re-layouts: 0.07 us -> 9.41 us  [the longest x7 6.96 us: columns(): return lax.dynamic_slice_in_dim(array, rank * own_width, own_width, 1)]
    slice x0 -> x16, local copies, waits for them, and re-layouts: none -> 5.32 us  [the longest x6 3.78 us: part(): piece[starts[index]:starts[index] + lengths[index]]]
    transpose x0 -> x9, local copies, waits for them, and re-layouts: none -> 4.62 us  [the longest x4 2.53 us: grad_out(): piece.reshape(part_rows, cot_width // own_width, own_width).swapaxes(0, 1)]
    reduce_scatter x2 -> x0, waiting for transfers between devices: 4.58 us -> none  [the longest x1 4.57 us: on_device(): lax.psum_scatter(grad_cols.astype(jnp.bfloat16), 'grp', scatter_dimension...]
    unnamed x51 -> x144, local copies, waits for them, and re-layouts: 10.3 us -> 14.7 us
  transfers between devices with their start and end apart: 3 -> 24, of which waited for: 1 -> 7; matrix products, arithmetic and copies ran while one was open for 17% -> 35% of each run, Pallas kernels for 0% -> 0%
where the time goes in v1:
time: 131 us; the launch traced here: 130 us
  local copies, waits for them, and re-layouts  38.1 us (29%)
  starting transfers between devices  34.3 us (26%)
  waiting for transfers between devices  29.3 us (22%)
  matrix products  17.3 us (13%)
  other arithmetic  9.11 us (7%)
  between operations  1.87 us (1%)
    ppermute x12, waiting for transfers between devices, shifted(): lax.ppermute(piece, axis, [(i, (i + shift) % size) for i in range(size)])  27.8 us
    ppermute x12, starting transfers between devices, shifted(): lax.ppermute(piece, axis, [(i, (i + shift) % size) for i in range(size)])  22 us
    unnamed x144, local copies, waits for them, and re-layouts  14.7 us
    ppermute x6, starting transfers between devices, plane_gather(): got[bit, shift] = lax.ppermute(piece, ('blk', 'tp'), pairs)  8.09 us
    dynamic_slice x7, local copies, waits for them, and re-layouts, columns(): return lax.dynamic_slice_in_dim(array, rank * own_width, own_width, 1)  6.96 us
    dot_general x1, matrix products, on_device_heads(): lax.dot_general(cot_rows, out_weight, (((1,), (1,)), ((), ())), preferred...  5 us
    slice x6, local copies, waits for them, and re-layouts, part(): piece[starts[index]:starts[index] + lengths[index]]  3.78 us
    ppermute x3, starting transfers between devices, on_device_heads(): piece = lax.ppermute(piece.astype(bf16), ('blk', 'tp'), pairs).astype(f32)  3.55 us
  transfers between devices with their start and end apart: 24, of which 7 were waited for; matrix products, arithmetic and copies ran while one was open for 35% of the time, Pallas kernels for 0%

profile of v1, /device:TPU:0, one launch (start us, length us, event | category | flops | bytes accessed | tf_op | source)
XLA Modules:
  0.0 130.0 jit_solution(7481602176118115813)
XLA Ops:
  0.7 3.1 %collective-permute-start.10 = (bf16[128,640]{1,0:T(8,128)(2,1)}, bf16[128,640]{1,0:T(8,128)(2,1)S(1)}, u32[]{:S(2)}, u32[]{:S(2)}) collective-permute-start(bf16[128,640]{1,0:T(8,128)(2,1)} %param.19), channel_id=1, source_target_pairs={{0,1},{1,0},{2,3},{3,2},{4,5},{5,4},{6,7},{7,6},{8,9},{9,8},{10,11... | collective-permute-start | bytes 491528 | tf_op jit(solution)/shard_map/ppermute | solution.py:204
  3.7 1.5 %collective-permute-start.12 = (bf16[128,640]{1,0:T(8,128)(2,1)}, bf16[128,640]{1,0:T(8,128)(2,1)S(1)}, u32[]{:S(2)}, u32[]{:S(2)}) collective-permute-start(bf16[128,640]{1,0:T(8,128)(2,1)} %param.19), channel_id=1, source_target_pairs={{0,4},{1,5},{2,6},{3,7},{4,0},{5,1},{6,2},{7,3},{8,12},{9,13},{10,... | collective-permute-start | bytes 491528 | tf_op jit(solution)/shard_map/ppermute | solution.py:204
  5.3 0.8 constant_dynamic-slice_fusion.18
  6.1 0.8 constant_dynamic-slice_fusion.17
  7.0 1.4 %constant_dynamic-slice_fusion.27 = (bf16[128,128]{1,0:T(8,128)(2,1)}, bf16[896,128]{1,0:T(8,128)(2,1)S(1)}, bf16[896,128]{1,0:T(8,128)(2,1)S(1)}, bf16[896,128]{1,0:T(8,128)(2,1)S(1)}) fusion(bf16[128,512]{1,0:T(8,128)(2,1)} %param.12, s32[]{:T(128)S(6)} %select_n.301, bf16[896,128]{1,0:T(8,128)(2,1)S(1)} %get-tuple-element.105, s32[]{:T(128)S(6)} %select_n.303, ...), kind=kLoop, calls=%fused_computation.206 | loop fusion | bytes 262160 | tf_op jit(solution)/shard_map/dynamic_slice | solution.py:240
  8.4 0.8 constant_dynamic-slice_fusion.15
  9.2 0.9 constant_dynamic-slice_fusion.14
  10.8 3.0 %collective-permute-start.1 = (bf16[896,128]{1,0:T(8,128)(2,1)S(1)}, bf16[896,128]{1,0:T(8,128)(2,1)S(1)}, u32[]{:S(2)}, u32[]{:S(2)}) collective-permute-start(bf16[896,128]{1,0:T(8,128)(2,1)S(1)} %get-tuple-element.80), channel_id=1, source_target_pairs={{0,16},{8,24},{16,0},{24,8},{1,17},{9,25},{17,1},{25,9},{2,18},{10... | collective-permute-start | bytes 688136 | tf_op jit(solution)/shard_map/ppermute | solution.py:184
  13.9 1.6 %collective-permute-start = (bf16[896,128]{1,0:T(8,128)(2,1)S(1)}, bf16[896,128]{1,0:T(8,128)(2,1)S(1)}, u32[]{:S(2)}, u32[]{:S(2)}) collective-permute-start(bf16[896,128]{1,0:T(8,128)(2,1)S(1)} %get-tuple-element.81), channel_id=1, source_target_pairs={{0,8},{8,16},{16,24},{24,0},{1,9},{9,17},{17,25},{25,1},{2,10},{10... | collective-permute-start | bytes 688136 | tf_op jit(solution)/shard_map/ppermute | solution.py:184
  15.8 2.3 %collective-permute-start.2 = (bf16[896,128]{1,0:T(8,128)(2,1)S(1)}, bf16[896,128]{1,0:T(8,128)(2,1)S(1)}, u32[]{:S(2)}, u32[]{:S(2)}) collective-permute-start(bf16[896,128]{1,0:T(8,128)(2,1)S(1)} %get-tuple-element.82), channel_id=1, source_target_pairs={{0,24},{8,0},{16,8},{24,16},{1,25},{9,1},{17,9},{25,17},{2,26},{10... | collective-permute-start | bytes 688136 | tf_op jit(solution)/shard_map/ppermute | solution.py:184
  18.8 10.8 %collective-permute-done.1 = bf16[896,128]{1,0:T(8,128)(2,1)S(1)} collective-permute-done((bf16[896,128]{1,0:T(8,128)(2,1)S(1)}, bf16[896,128]{1,0:T(8,128)(2,1)S(1)}, u32[]{:S(2)}, u32[]{:S(2)}) %collective-permute-start.1) | collective-permute-done | bytes 229408 | tf_op jit(solution)/shard_map/ppermute | solution.py:184
  34.6 1.0 copy-done
  36.2 1.3 maximum_select_fusion
  37.5 1.8 %copy.52 = bf16[128,8,640]{0,2,1:T(8,128)(2,1)S(1)} copy(bf16[128,8,640]{2,0,1:T(8,128)(2,1)} %bitcast.281) | data formatting | bytes 2621440 | tf_op jit(solution)/shard_map/transpose | solution.py:251
  39.2 5.0 %convolution_convert_fusion.3 = bf16[128,512]{1,0:T(8,128)(2,1)} fusion(bf16[128,5120]{0,1:T(8,128)(2,1)S(1)} %bitcast.278, bf16[512,5120]{1,0:T(8,128)(2,1)} %param.18), kind=kOutput, calls=%fused_computation.26 | convolution fusion | flops 671154176 | bytes 6684672 | tf_op jit(solution)/shard_map/dot_general | solution.py:252
  44.2 1.4 %fusion.65 = (bf16[16,1280]{0,1:T(8,128)(2,1)}, bf16[16,1280]{0,1:T(8,128)(2,1)}, bf16[16,1280]{0,1:T(8,128)(2,1)S(1)}, bf16[16,1280]{0,1:T(8,128)(2,1)S(1)}) fusion(bf16[128,5120]{0,1:T(8,128)(2,1)S(1)} %bitcast.279, s32[]{:T(128)S(6)} %select_n.345, s32[]{:T(128)S(6)} %select_n.357, s32[]{:T(128)S(6)} %select_n.351, s32[]{:T(128)S(6)} %select_n.349, ...), kind=kLoop, calls=%fused_computation.233 | loop fusion | bytes 327700 | tf_op jit(solution)/shard_map/dynamic_slice | solution.py:261
  45.6 1.1 copy.61
  46.7 1.1 copy.58
  47.8 1.4 %constant_dynamic-slice_fusion.9 = (bf16[128,128]{1,0:T(8,128)(2,1)}, bf16[128,128]{1,0:T(8,128)(2,1)S(1)}, bf16[128,128]{1,0:T(8,128)(2,1)S(1)}, bf16[128,128]{1,0:T(8,128)(2,1)S(1)}) fusion(bf16[128,512]{1,0:T(8,128)(2,1)} %convolution_convert_fusion.3, s32[]{:T(128)S(6)} %select_n.301, s32[]{:T(128)S(6)} %select_n.307, s32[]{:T(128)S(6)} %select_n.305, ...), kind=kLoop, calls=%fused_computation.188 | loop fusion | bytes 262160 | tf_op jit(solution)/shard_map/dynamic_slice | solution.py:240
  49.6 3.2 %collective-permute-start.14 = (bf16[288,128]{1,0:T(8,128)(2,1)S(1)}, bf16[288,128]{1,0:T(8,128)(2,1)S(1)}, u32[]{:S(2)}, u32[]{:S(2)}) collective-permute-start(bf16[288,128]{1,0:T(8,128)(2,1)S(1)} %pad_maximum_fusion.7), channel_id=1, source_target_pairs={{0,8},{8,16},{16,24},{24,0},{1,9},{9,17},{17,25},{25,1},{2,10},{10... | collective-permute-start | bytes 221192 | tf_op jit(solution)/shard_map/ppermute | solution.py:184
  53.5 3.3 %collective-permute-start.15 = (bf16[288,128]{1,0:T(8,128)(2,1)S(1)}, bf16[288,128]{1,0:T(8,128)(2,1)S(1)}, u32[]{:S(2)}, u32[]{:S(2)}) collective-permute-start(bf16[288,128]{1,0:T(8,128)(2,1)S(1)} %pad_maximum_fusion.8), channel_id=1, source_target_pairs={{0,16},{8,24},{16,0},{24,8},{1,17},{9,25},{17,1},{25,9},{2,18},{10... | collective-permute-start | bytes 221192 | tf_op jit(solution)/shard_map/ppermute | solution.py:184
  56.8 0.9 collective-permute-done.16
  57.6 4.2 %collective-permute-done.15 = bf16[288,128]{1,0:T(8,128)(2,1)S(1)} collective-permute-done((bf16[288,128]{1,0:T(8,128)(2,1)S(1)}, bf16[288,128]{1,0:T(8,128)(2,1)S(1)}, u32[]{:S(2)}, u32[]{:S(2)}) %collective-permute-start.15) | collective-permute-done | bytes 73760 | tf_op jit(solution)/shard_map/ppermute | solution.py:184
  62.1 0.7 copy.88
  62.8 1.5 %collective-permute-start.22 = (bf16[64,1280]{1,0:T(8,128)(2,1)}, bf16[64,1280]{1,0:T(8,128)(2,1)}, u32[]{:S(2)}, u32[]{:S(2)}) collective-permute-start(bf16[64,1280]{1,0:T(8,128)(2,1)} %bitcast.273), channel_id=1, source_target_pairs={{0,4},{1,5},{2,6},{3,7},{4,0},{5,1},{6,2},{7,3},{8,12},{9,13},{10,... | collective-permute-start | bytes 491528 | tf_op jit(solution)/shard_map/ppermute | solution.py:204
  64.3 1.5 %collective-permute-start.21 = (bf16[64,1280]{1,0:T(8,128)(2,1)}, bf16[64,1280]{1,0:T(8,128)(2,1)}, u32[]{:S(2)}, u32[]{:S(2)}) collective-permute-start(bf16[64,1280]{1,0:T(8,128)(2,1)} %bitcast.273), channel_id=1, source_target_pairs={{0,5},{1,4},{2,7},{3,6},{4,1},{5,0},{6,3},{7,2},{8,13},{9,12},{10,... | collective-permute-start | bytes 491528 | tf_op jit(solution)/shard_map/ppermute | solution.py:204
  66.4 1.0 fusion.10
  68.6 1.0 fusion.11
  69.6 0.9 fusion.12
  70.5 0.7 multiply_reduce_fusion
  74.3 3.8 %collective-permute-start.3 = (bf16[512,128]{1,0:T(8,128)(2,1)S(1)}, bf16[512,128]{1,0:T(8,128)(2,1)S(1)}, u32[]{:S(2)}, u32[]{:S(2)}) collective-permute-start(bf16[512,128]{1,0:T(8,128)(2,1)S(1)} %bitcast.294), channel_id=1, source_target_pairs={{0,24},{8,0},{16,8},{24,16},{1,25},{9,1},{17,9},{25,17},{2,26},{10... | collective-permute-start | bytes 393224 | tf_op jit(solution)/shard_map/ppermute | solution.py:184
  78.4 0.8 concatenate.105
  79.4 0.8 concatenate.104
  80.2 0.8 concatenate.103
  80.9 0.7 bitcast_dynamic-update-slice_fusion.6
  81.7 1.4 %collective-permute-start.4 = (bf16[512,128]{1,0:T(8,128)(2,1)S(1)}, bf16[512,128]{1,0:T(8,128)(2,1)S(1)}, u32[]{:S(2)}, u32[]{:S(2)}) collective-permute-start(bf16[512,128]{1,0:T(8,128)(2,1)S(1)} %bitcast.295), channel_id=1, source_target_pairs={{0,16},{8,24},{16,0},{24,8},{1,17},{9,25},{17,1},{25,9},{2,18},{10... | collective-permute-start | bytes 393224 | tf_op jit(solution)/shard_map/ppermute | solution.py:184
  83.1 6.1 %collective-permute-done.4 = bf16[512,128]{1,0:T(8,128)(2,1)S(1)} collective-permute-done((bf16[512,128]{1,0:T(8,128)(2,1)S(1)}, bf16[512,128]{1,0:T(8,128)(2,1)S(1)}, u32[]{:S(2)}, u32[]{:S(2)}) %collective-permute-start.4) | collective-permute-done | bytes 131104 | tf_op jit(solution)/shard_map/ppermute | solution.py:184
  89.2 2.0 %collective-permute-start.17 = (bf16[896,128]{0,1:T(8,128)(2,1)}, bf16[896,128]{0,1:T(8,128)(2,1)}, u32[]{:S(2)}, u32[]{:S(2)}) collective-permute-start(bf16[896,128]{0,1:T(8,128)(2,1)} %concatenate.103), channel_id=1, source_target_pairs={{0,24},{8,0},{16,8},{24,16},{1,25},{9,1},{17,9},{25,17},{2,26},{10... | collective-permute-start | bytes 688136 | tf_op jit(solution)/shard_map/ppermute | solution.py:184
  91.7 3.4 %convolution_convert_fusion = bf16[128,5120]{1,0:T(8,128)(2,1)S(1)} fusion(bf16[128,512]{0,1:T(8,128)(2,1)S(1)} %bitcast.302, bf16[512,5120]{1,0:T(8,128)(2,1)} %param.18), kind=kOutput, calls=%fused_computation | convolution fusion | flops 671744000 | bytes 6684672 | tf_op jit(solution)/shard_map/dot_general | solution.py:347
  95.4 1.0 reshape.414
  96.4 0.9 constant_dynamic-slice_fusion.12
  97.3 0.9 copy.87
  98.9 1.3 %fusion.22 = bf16[2,64,1280]{2,1,0:T(8,128)(2,1)S(1)} fusion(s32[]{:T(128)S(6)} %select_n.338, bf16[1,64,1280]{2,1,0:T(8,128)(2,1)} %bitcast.126, bf16[1,64,1280]{2,1,0:T(8,128)(2,1)} %bitcast.127), kind=kLoop, calls=%fused_computation.62 | loop fusion | flops 491520 | bytes 655364 | tf_op jit(solution)/shard_map/stack | solution.py:179
  100.2 1.2 fusion.25
  102.0 1.0 bitcast_dynamic-update-slice_fusion.4
  103.0 5.8 %collective-permute-done.18 = bf16[896,128]{0,1:T(8,128)(2,1)} collective-permute-done((bf16[896,128]{0,1:T(8,128)(2,1)}, bf16[896,128]{0,1:T(8,128)(2,1)}, u32[]{:S(2)}, u32[]{:S(2)}) %collective-permute-start.18) | collective-permute-done | bytes 229408 | tf_op jit(solution)/shard_map/ppermute | solution.py:184
  108.8 1.0 bitcast_dynamic-update-slice_fusion.2
  109.8 1.0 bitcast_dynamic-update-slice_fusion.5
  110.8 1.0 bitcast_dynamic-update-slice_fusion.3
  111.8 1.2 copy-done.3
  113.2 0.8 copy.72
  114.0 0.8 copy.71
  114.8 1.1 constant_dynamic-slice_fusion.3
  115.9 0.8 copy.70
  116.7 0.8 copy.69
  117.5 0.8 copy.68
  118.3 0.8 copy.67
  119.0 1.2 bitcast_add_fusion
  120.3 1.5 %collective-permute-start.7 = (bf16[128,640]{1,0:T(8,128)(2,1)S(1)}, bf16[128,640]{1,0:T(8,128)(2,1)S(1)}, u32[]{:S(2)}, u32[]{:S(2)}) collective-permute-start(bf16[128,640]{1,0:T(8,128)(2,1)S(1)} %get-tuple-element.44), channel_id=1, source_target_pairs={{0,1},{1,0},{2,3},{3,2},{4,5},{5,4},{6,7},{7,6},{8,9},{9,8},{10,11... | collective-permute-start | bytes 491528 | tf_op jit(solution)/shard_map/ppermute | solution.py:364
  121.8 1.4 %collective-permute-start.9 = (bf16[128,640]{1,0:T(8,128)(2,1)S(1)}, bf16[128,640]{1,0:T(8,128)(2,1)S(1)}, u32[]{:S(2)}, u32[]{:S(2)}) collective-permute-start(bf16[128,640]{1,0:T(8,128)(2,1)S(1)} %get-tuple-element.45), channel_id=1, source_target_pairs={{0,5},{1,4},{2,7},{3,6},{4,1},{5,0},{6,3},{7,2},{8,13},{9,12},{10,... | collective-permute-start | bytes 491528 | tf_op jit(solution)/shard_map/ppermute | solution.py:364
  123.8 1.5 %maximum_select_fusion.1 = bf16[2,2,2,64,1280]{4,3,2,1,0:T(8,128)(2,1)S(1)} fusion(bf16[2,1,2,64,1280]{4,3,2,1,0:T(8,128)(2,1)} %bitcast.131, bf16[2,1,2,64,1280]{4,3,2,1,0:T(8,128)(2,1)S(1)} %bitcast.285, pred[]{:T(512)S(6)} %eq.66), kind=kLoop, calls=%fused_computation.10 | loop fusion | flops 1966080 | bytes 2621441 | tf_op jit(solution)/shard_map/jit(_where)/select_n | solution.py:218
  125.4 2.3 %fusion.74 = f32[512,1280]{1,0:T(8,128)} fusion(bf16[512,512]{1,0:T(8,128)(2,1)S(1)} %bitcast.283, bf16[512,1280]{1,0:T(8,128)(2,1)S(1)} %bitcast.282), kind=kOutput, calls=%fused_computation.242 | convolution fusion | flops 671088640 | bytes 4456448 | tf_op jit(solution)/shard_map/gtf,tc->gfc/dot_general | solution.py:344
  128.2 1.1 collective-permute-done.8
  129.2 0.7 fusion.34
  (215 shorter events, 16.5 us)
Async XLA Ops:
  0.6 17.4 %copy-start.26 = (bf16[128,640]{1,0:T(8,128)(2,1)S(1)}, bf16[128,640]{1,0:T(8,128)(2,1)}, u32[]{:S(2)}) copy-start(bf16[128,640]{1,0:T(8,128)(2,1)} %param.19) | copy-start | bytes 491524
  0.6 9.5 %copy-start.13 = (bf16[192,512]{1,0:T(8,128)(2,1)S(1)}, bf16[192,512]{1,0:T(8,128)(2,1)}, u32[]{:S(2)}) copy-start(bf16[192,512]{1,0:T(8,128)(2,1)} %param.15) | copy-start | bytes 589828
  0.7 14.9 %copy-start.53 = (s32[512]{0:T(512)S(1)}, s32[512]{0:T(512)}, u32[]{:S(2)}) copy-start(s32[512]{0:T(512)} %param.17) | copy-start | bytes 6148
  0.7 14.9 %copy-start.52 = (s32[512]{0:T(512)S(1)}, s32[512]{0:T(512)}, u32[]{:S(2)}) copy-start(s32[512]{0:T(512)} %param.16) | copy-start | bytes 6148
  0.7 15.1 %collective-permute-start.10 = (bf16[128,640]{1,0:T(8,128)(2,1)}, bf16[128,640]{1,0:T(8,128)(2,1)S(1)}, u32[]{:S(2)}, u32[]{:S(2)}) collective-permute-start(bf16[128,640]{1,0:T(8,128)(2,1)} %param.19), channel_id=1, source_target_pairs={{0,1},{1,0},{2,3},{3,2},{4,5},{5,4},{6,7},{7,6},{8,9},{9,8},{10,11... | collective-permute-start | bytes 491528 | tf_op jit(solution)/shard_map/ppermute | solution.py:204
  3.7 14.6 %collective-permute-start.12 = (bf16[128,640]{1,0:T(8,128)(2,1)}, bf16[128,640]{1,0:T(8,128)(2,1)S(1)}, u32[]{:S(2)}, u32[]{:S(2)}) collective-permute-start(bf16[128,640]{1,0:T(8,128)(2,1)} %param.19), channel_id=1, source_target_pairs={{0,4},{1,5},{2,6},{3,7},{4,0},{5,1},{6,2},{7,3},{8,12},{9,13},{10,... | collective-permute-start | bytes 491528 | tf_op jit(solution)/shard_map/ppermute | solution.py:204
  5.2 13.1 %collective-permute-start.11 = (bf16[128,640]{1,0:T(8,128)(2,1)}, bf16[128,640]{1,0:T(8,128)(2,1)S(1)}, u32[]{:S(2)}, u32[]{:S(2)}) collective-permute-start(bf16[128,640]{1,0:T(8,128)(2,1)} %param.19), channel_id=1, source_target_pairs={{0,5},{1,4},{2,7},{3,6},{4,1},{5,0},{6,3},{7,2},{8,13},{9,12},{10,... | collective-permute-start | bytes 491528 | tf_op jit(solution)/shard_map/ppermute | solution.py:204
  6.1 28.0 %copy-start.33 = (bf16[128,128]{1,0:T(8,128)(2,1)}, bf16[128,128]{1,0:T(8,128)(2,1)S(1)}, u32[]{:S(2)}) copy-start(bf16[128,128]{1,0:T(8,128)(2,1)S(1)} %get-tuple-element.99) | copy-start | bytes 98308
  6.9 27.1 %copy-start.35 = (bf16[128,128]{1,0:T(8,128)(2,1)}, bf16[128,128]{1,0:T(8,128)(2,1)S(1)}, u32[]{:S(2)}) copy-start(bf16[128,128]{1,0:T(8,128)(2,1)S(1)} %get-tuple-element.103) | copy-start | bytes 98308
  9.2 24.3 %copy-start.4 = (bf16[128,128]{1,0:T(8,128)(2,1)}, bf16[128,128]{1,0:T(8,128)(2,1)S(1)}, u32[]{:S(2)}) copy-start(bf16[128,128]{1,0:T(8,128)(2,1)S(1)} %get-tuple-element.111) | copy-start | bytes 98308
  10.2 23.3 %copy-start.15 = (bf16[192,128]{1,0:T(8,128)(2,1)}, bf16[192,128]{1,0:T(8,128)(2,1)S(1)}, u32[]{:S(2)}) copy-start(bf16[192,128]{1,0:T(8,128)(2,1)S(1)} %get-tuple-element.75) | copy-start | bytes 147460
  10.8 18.8 %collective-permute-start.1 = (bf16[896,128]{1,0:T(8,128)(2,1)S(1)}, bf16[896,128]{1,0:T(8,128)(2,1)S(1)}, u32[]{:S(2)}, u32[]{:S(2)}) collective-permute-start(bf16[896,128]{1,0:T(8,128)(2,1)S(1)} %get-tuple-element.80), channel_id=1, source_target_pairs={{0,16},{8,24},{16,0},{24,8},{1,17},{9,25},{17,1},{25,9},{2,18},{10... | collective-permute-start | bytes 688136 | tf_op jit(solution)/shard_map/ppermute | solution.py:184
  13.9 17.1 %collective-permute-start = (bf16[896,128]{1,0:T(8,128)(2,1)S(1)}, bf16[896,128]{1,0:T(8,128)(2,1)S(1)}, u32[]{:S(2)}, u32[]{:S(2)}) collective-permute-start(bf16[896,128]{1,0:T(8,128)(2,1)S(1)} %get-tuple-element.81), channel_id=1, source_target_pairs={{0,8},{8,16},{16,24},{24,0},{1,9},{9,17},{17,25},{25,1},{2,10},{10... | collective-permute-start | bytes 688136 | tf_op jit(solution)/shard_map/ppermute | solution.py:184
  15.8 16.5 %collective-permute-start.2 = (bf16[896,128]{1,0:T(8,128)(2,1)S(1)}, bf16[896,128]{1,0:T(8,128)(2,1)S(1)}, u32[]{:S(2)}, u32[]{:S(2)}) collective-permute-start(bf16[896,128]{1,0:T(8,128)(2,1)S(1)} %get-tuple-element.82), channel_id=1, source_target_pairs={{0,24},{8,0},{16,8},{24,16},{1,25},{9,1},{17,9},{25,17},{2,26},{10... | collective-permute-start | bytes 688136 | tf_op jit(solution)/shard_map/ppermute | solution.py:184
  18.7 17.4 %collective-permute-start.13 = (bf16[2,2,128,640]{3,2,1,0:T(8,128)(2,1)S(1)}, bf16[2,2,128,640]{3,2,1,0:T(8,128)(2,1)S(1)}, u32[]{:S(2)}, u32[]{:S(2)}) collective-permute-start(bf16[2,2,128,640]{3,2,1,0:T(8,128)(2,1)S(1)} %bitcast.286), channel_id=1, source_target_pairs={{0,2},{2,0},{4,6},{6,4},{1,3},{3,1},{5,7},{7,5},{8,10},{10,8},{12,... | collective-permute-start | bytes 1966088 | tf_op jit(solution)/shard_map/ppermute | solution.py:188
  30.3 3.7 %copy-start.19 = (bf16[192,128]{1,0:T(8,128)(2,1)}, bf16[192,128]{1,0:T(8,128)(2,1)S(1)}, u32[]{:S(2)}) copy-start(bf16[192,128]{1,0:T(8,128)(2,1)S(1)} %get-tuple-element.63) | copy-start | bytes 147460
  30.9 3.0 %copy-start.6 = (bf16[128,128]{1,0:T(8,128)(2,1)}, bf16[128,128]{1,0:T(8,128)(2,1)S(1)}, u32[]{:S(2)}) copy-start(bf16[128,128]{1,0:T(8,128)(2,1)S(1)} %get-tuple-element.54) | copy-start | bytes 98308
  30.9 3.6 %copy-start.40 = (bf16[128,128]{1,0:T(8,128)(2,1)}, bf16[128,128]{1,0:T(8,128)(2,1)S(1)}, u32[]{:S(2)}) copy-start(bf16[128,128]{1,0:T(8,128)(2,1)S(1)} %get-tuple-element.55) | copy-start | bytes 98308
  30.9 3.6 %copy-start.42 = (bf16[128,128]{1,0:T(8,128)(2,1)}, bf16[128,128]{1,0:T(8,128)(2,1)S(1)}, u32[]{:S(2)}) copy-start(bf16[128,128]{1,0:T(8,128)(2,1)S(1)} %get-tuple-element.53) | copy-start | bytes 98308
  31.6 2.4 %copy-start.22 = (bf16[192,128]{1,0:T(8,128)(2,1)}, bf16[192,128]{1,0:T(8,128)(2,1)S(1)}, u32[]{:S(2)}) copy-start(bf16[192,128]{1,0:T(8,128)(2,1)S(1)} %get-tuple-element.61) | copy-start | bytes 147460
  32.2 1.8 %copy-start.8 = (bf16[128,128]{1,0:T(8,128)(2,1)}, bf16[128,128]{1,0:T(8,128)(2,1)S(1)}, u32[]{:S(2)}) copy-start(bf16[128,128]{1,0:T(8,128)(2,1)S(1)} %get-tuple-element.50) | copy-start | bytes 98308
  32.2 2.4 %copy-start.44 = (bf16[128,128]{1,0:T(8,128)(2,1)}, bf16[128,128]{1,0:T(8,128)(2,1)S(1)}, u32[]{:S(2)}) copy-start(bf16[128,128]{1,0:T(8,128)(2,1)S(1)} %get-tuple-element.51) | copy-start | bytes 98308
  32.2 2.4 %copy-start.46 = (bf16[128,128]{1,0:T(8,128)(2,1)}, bf16[128,128]{1,0:T(8,128)(2,1)S(1)}, u32[]{:S(2)}) copy-start(bf16[128,128]{1,0:T(8,128)(2,1)S(1)} %get-tuple-element.49) | copy-start | bytes 98308
  32.9 1.1 copy-start.24
  33.5 1.1 copy-start.48
  33.5 1.1 copy-start.50
  49.4 16.9 %copy-start.1 = (f32[512,512]{0,1:T(8,128)S(1)}, f32[512,512]{0,1:T(8,128)}, u32[]{:S(2)}) copy-start(f32[512,512]{0,1:T(8,128)} %copy-done) | copy-start | bytes 3145732
  49.4 16.9 %copy-start.30 = (bf16[128,128]{1,0:T(8,128)(2,1)S(1)}, bf16[128,128]{1,0:T(8,128)(2,1)}, u32[]{:S(2)}) copy-start(bf16[128,128]{1,0:T(8,128)(2,1)} %get-tuple-element.115) | copy-start | bytes 98308
  49.6 12.2 %collective-permute-start.14 = (bf16[288,128]{1,0:T(8,128)(2,1)S(1)}, bf16[288,128]{1,0:T(8,128)(2,1)S(1)}, u32[]{:S(2)}, u32[]{:S(2)}) collective-permute-start(bf16[288,128]{1,0:T(8,128)(2,1)S(1)} %pad_maximum_fusion.7), channel_id=1, source_target_pairs={{0,8},{8,16},{16,24},{24,0},{1,9},{9,17},{17,25},{25,1},{2,10},{10... | collective-permute-start | bytes 221192 | tf_op jit(solution)/shard_map/ppermute | solution.py:184
  52.8 4.8 %collective-permute-start.16 = (bf16[288,128]{1,0:T(8,128)(2,1)S(1)}, bf16[288,128]{1,0:T(8,128)(2,1)S(1)}, u32[]{:S(2)}, u32[]{:S(2)}) collective-permute-start(bf16[288,128]{1,0:T(8,128)(2,1)S(1)} %pad_maximum_fusion.9), channel_id=1, source_target_pairs={{0,24},{8,0},{16,8},{24,16},{1,25},{9,1},{17,9},{25,17},{2,26},{10... | collective-permute-start | bytes 221192 | tf_op jit(solution)/shard_map/ppermute | solution.py:184
  53.5 8.3 %collective-permute-start.15 = (bf16[288,128]{1,0:T(8,128)(2,1)S(1)}, bf16[288,128]{1,0:T(8,128)(2,1)S(1)}, u32[]{:S(2)}, u32[]{:S(2)}) collective-permute-start(bf16[288,128]{1,0:T(8,128)(2,1)S(1)} %pad_maximum_fusion.8), channel_id=1, source_target_pairs={{0,16},{8,24},{16,0},{24,8},{1,17},{9,25},{17,1},{25,9},{2,18},{10... | collective-permute-start | bytes 221192 | tf_op jit(solution)/shard_map/ppermute | solution.py:184
  62.8 35.4 %collective-permute-start.22 = (bf16[64,1280]{1,0:T(8,128)(2,1)}, bf16[64,1280]{1,0:T(8,128)(2,1)}, u32[]{:S(2)}, u32[]{:S(2)}) collective-permute-start(bf16[64,1280]{1,0:T(8,128)(2,1)} %bitcast.273), channel_id=1, source_target_pairs={{0,4},{1,5},{2,6},{3,7},{4,0},{5,1},{6,2},{7,3},{8,12},{9,13},{10,... | collective-permute-start | bytes 491528 | tf_op jit(solution)/shard_map/ppermute | solution.py:204
  64.3 34.5 %collective-permute-start.21 = (bf16[64,1280]{1,0:T(8,128)(2,1)}, bf16[64,1280]{1,0:T(8,128)(2,1)}, u32[]{:S(2)}, u32[]{:S(2)}) collective-permute-start(bf16[64,1280]{1,0:T(8,128)(2,1)} %bitcast.273), channel_id=1, source_target_pairs={{0,5},{1,4},{2,7},{3,6},{4,1},{5,0},{6,3},{7,2},{8,13},{9,12},{10,... | collective-permute-start | bytes 491528 | tf_op jit(solution)/shard_map/ppermute | solution.py:204
  65.8 34.3 %collective-permute-start.20 = (bf16[64,1280]{1,0:T(8,128)(2,1)}, bf16[64,1280]{1,0:T(8,128)(2,1)}, u32[]{:S(2)}, u32[]{:S(2)}) collective-permute-start(bf16[64,1280]{1,0:T(8,128)(2,1)} %bitcast.273), channel_id=1, source_target_pairs={{0,1},{1,0},{2,3},{3,2},{4,5},{5,4},{6,7},{7,6},{8,9},{9,8},{10,11... | collective-permute-start | bytes 491528 | tf_op jit(solution)/shard_map/ppermute | solution.py:204
  66.4 1.0 copy-start.32
  67.8 1.8 %copy-start.36 = (bf16[128,128]{1,0:T(8,128)(2,1)S(1)}, bf16[128,128]{1,0:T(8,128)(2,1)}, u32[]{:S(2)}) copy-start(bf16[128,128]{1,0:T(8,128)(2,1)} %copy-done.35) | copy-start | bytes 98308
  67.8 1.7 %copy-start.41 = (bf16[128,128]{1,0:T(8,128)(2,1)S(1)}, bf16[128,128]{1,0:T(8,128)(2,1)}, u32[]{:S(2)}) copy-start(bf16[128,128]{1,0:T(8,128)(2,1)} %copy-done.40) | copy-start | bytes 98308
  67.8 1.7 %copy-start.45 = (bf16[128,128]{1,0:T(8,128)(2,1)S(1)}, bf16[128,128]{1,0:T(8,128)(2,1)}, u32[]{:S(2)}) copy-start(bf16[128,128]{1,0:T(8,128)(2,1)} %copy-done.44) | copy-start | bytes 98308
  67.8 1.7 %copy-start.49 = (bf16[128,128]{1,0:T(8,128)(2,1)S(1)}, bf16[128,128]{1,0:T(8,128)(2,1)}, u32[]{:S(2)}) copy-start(bf16[128,128]{1,0:T(8,128)(2,1)} %copy-done.48) | copy-start | bytes 98308
  67.8 2.6 %copy-start.14 = (bf16[192,128]{1,0:T(8,128)(2,1)S(1)}, bf16[192,128]{1,0:T(8,128)(2,1)}, u32[]{:S(2)}) copy-start(bf16[192,128]{1,0:T(8,128)(2,1)} %get-tuple-element.79) | copy-start | bytes 147460
  67.8 2.6 %copy-start.17 = (bf16[192,128]{1,0:T(8,128)(2,1)S(1)}, bf16[192,128]{1,0:T(8,128)(2,1)}, u32[]{:S(2)}) copy-start(bf16[192,128]{1,0:T(8,128)(2,1)} %get-tuple-element.64) | copy-start | bytes 147460
  67.9 2.6 %copy-start.18 = (bf16[192,128]{1,0:T(8,128)(2,1)S(1)}, bf16[192,128]{1,0:T(8,128)(2,1)}, u32[]{:S(2)}) copy-start(bf16[192,128]{1,0:T(8,128)(2,1)} %get-tuple-element.62) | copy-start | bytes 147460
  67.9 2.6 %copy-start.21 = (bf16[192,128]{1,0:T(8,128)(2,1)S(1)}, bf16[192,128]{1,0:T(8,128)(2,1)}, u32[]{:S(2)}) copy-start(bf16[192,128]{1,0:T(8,128)(2,1)} %get-tuple-element.66) | copy-start | bytes 147460
  71.2 1.3 copy-start.5
  71.2 1.3 copy-start.7
  71.2 1.3 copy-start.9
  71.3 1.3 copy-start.11
  73.5 4.6 %copy-start.27 = (bf16[512,1,128]{0,2,1:T(8,128)(2,1)S(1)}, bf16[512,1,128]{0,2,1:T(8,128)(2,1)}, u32[]{:S(2)}) copy-start(bf16[512,1,128]{0,2,1:T(8,128)(2,1)} %fusion.10) | copy-start | bytes 393220
  73.6 4.6 %copy-start.29 = (bf16[512,1,128]{0,2,1:T(8,128)(2,1)S(1)}, bf16[512,1,128]{0,2,1:T(8,128)(2,1)}, u32[]{:S(2)}) copy-start(bf16[512,1,128]{0,2,1:T(8,128)(2,1)} %fusion.12) | copy-start | bytes 393220
  73.9 4.3 %copy-start.28 = (bf16[512,1,128]{0,2,1:T(8,128)(2,1)S(1)}, bf16[512,1,128]{0,2,1:T(8,128)(2,1)}, u32[]{:S(2)}) copy-start(bf16[512,1,128]{0,2,1:T(8,128)(2,1)} %fusion.11) | copy-start | bytes 393220
  74.2 17.0 %collective-permute-start.5 = (bf16[512,128]{1,0:T(8,128)(2,1)S(1)}, bf16[512,128]{1,0:T(8,128)(2,1)S(1)}, u32[]{:S(2)}, u32[]{:S(2)}) collective-permute-start(bf16[512,128]{1,0:T(8,128)(2,1)S(1)} %bitcast.293), channel_id=1, source_target_pairs={{0,8},{8,16},{16,24},{24,0},{1,9},{9,17},{17,25},{25,1},{2,10},{10... | collective-permute-start | bytes 393224 | tf_op jit(solution)/shard_map/ppermute | solution.py:184
  74.3 7.3 %collective-permute-start.3 = (bf16[512,128]{1,0:T(8,128)(2,1)S(1)}, bf16[512,128]{1,0:T(8,128)(2,1)S(1)}, u32[]{:S(2)}, u32[]{:S(2)}) collective-permute-start(bf16[512,128]{1,0:T(8,128)(2,1)S(1)} %bitcast.294), channel_id=1, source_target_pairs={{0,24},{8,0},{16,8},{24,16},{1,25},{9,1},{17,9},{25,17},{2,26},{10... | collective-permute-start | bytes 393224 | tf_op jit(solution)/shard_map/ppermute | solution.py:184
  81.7 7.6 %collective-permute-start.4 = (bf16[512,128]{1,0:T(8,128)(2,1)S(1)}, bf16[512,128]{1,0:T(8,128)(2,1)S(1)}, u32[]{:S(2)}, u32[]{:S(2)}) collective-permute-start(bf16[512,128]{1,0:T(8,128)(2,1)S(1)} %bitcast.295), channel_id=1, source_target_pairs={{0,16},{8,24},{16,0},{24,8},{1,17},{9,25},{17,1},{25,9},{2,18},{10... | collective-permute-start | bytes 393224 | tf_op jit(solution)/shard_map/ppermute | solution.py:184
  89.2 12.8 %collective-permute-start.17 = (bf16[896,128]{0,1:T(8,128)(2,1)}, bf16[896,128]{0,1:T(8,128)(2,1)}, u32[]{:S(2)}, u32[]{:S(2)}) collective-permute-start(bf16[896,128]{0,1:T(8,128)(2,1)} %concatenate.103), channel_id=1, source_target_pairs={{0,24},{8,0},{16,8},{24,16},{1,25},{9,1},{17,9},{25,17},{2,26},{10... | collective-permute-start | bytes 688136 | tf_op jit(solution)/shard_map/ppermute | solution.py:184
  91.3 17.5 %collective-permute-start.18 = (bf16[896,128]{0,1:T(8,128)(2,1)}, bf16[896,128]{0,1:T(8,128)(2,1)}, u32[]{:S(2)}, u32[]{:S(2)}) collective-permute-start(bf16[896,128]{0,1:T(8,128)(2,1)} %concatenate.104), channel_id=1, source_target_pairs={{0,16},{8,24},{16,0},{24,8},{1,17},{9,25},{17,1},{25,9},{2,18},{10... | collective-permute-start | bytes 688136 | tf_op jit(solution)/shard_map/ppermute | solution.py:184
  96.4 1.9 %copy-start.12 = (bf16[896,128]{0,1:T(8,128)(2,1)S(1)}, bf16[896,128]{0,1:T(8,128)(2,1)}, u32[]{:S(2)}) copy-start(bf16[896,128]{0,1:T(8,128)(2,1)} %concatenate.105) | copy-start | bytes 688132
  98.3 3.8 %copy-start.2 = (bf16[8,896,128]{1,2,0:T(8,128)(2,1)S(1)}, bf16[8,896,128]{1,2,0:T(8,128)(2,1)}, u32[]{:S(2)}) copy-start(bf16[8,896,128]{1,2,0:T(8,128)(2,1)} %bitcast_dynamic-update-slice_fusion.6) | copy-start | bytes 5505028
  98.3 11.5 %collective-permute-start.19 = (bf16[896,128]{0,1:T(8,128)(2,1)S(1)}, bf16[896,128]{0,1:T(8,128)(2,1)S(1)}, u32[]{:S(2)}, u32[]{:S(2)}) collective-permute-start(bf16[896,128]{0,1:T(8,128)(2,1)S(1)} %copy-done.12), channel_id=1, source_target_pairs={{0,8},{8,16},{16,24},{24,0},{1,9},{9,17},{17,25},{25,1},{2,10},{10... | collective-permute-start | bytes 688136 | tf_op jit(solution)/shard_map/ppermute | solution.py:184
  98.9 20.2 %collective-permute-start.6 = (bf16[2,2,128,640]{3,2,1,0:T(8,128)(2,1)}, bf16[2,2,128,640]{3,2,1,0:T(8,128)(2,1)}, u32[]{:S(2)}, u32[]{:S(2)}) collective-permute-start(bf16[2,2,128,640]{3,2,1,0:T(8,128)(2,1)} %bitcast.272), channel_id=1, source_target_pairs={{0,2},{2,0},{4,6},{6,4},{1,3},{3,1},{5,7},{7,5},{8,10},{10,8},{12,... | collective-permute-start | bytes 1966088 | tf_op jit(solution)/shard_map/ppermute | solution.py:188
  101.5 22.4 %collective-permute-start.23 = (bf16[2,2,64,1280]{3,2,1,0:T(8,128)(2,1)S(1)}, bf16[2,2,64,1280]{3,2,1,0:T(8,128)(2,1)}, u32[]{:S(2)}, u32[]{:S(2)}) collective-permute-start(bf16[2,2,64,1280]{3,2,1,0:T(8,128)(2,1)S(1)} %bitcast.284), channel_id=1, source_target_pairs={{0,2},{2,0},{4,6},{6,4},{1,3},{3,1},{5,7},{7,5},{8,10},{10,8},{12,... | collective-permute-start | bytes 1966088 | tf_op jit(solution)/shard_map/ppermute | solution.py:188
  111.8 1.2 copy-start.3
  120.3 7.5 %collective-permute-start.7 = (bf16[128,640]{1,0:T(8,128)(2,1)S(1)}, bf16[128,640]{1,0:T(8,128)(2,1)S(1)}, u32[]{:S(2)}, u32[]{:S(2)}) collective-permute-start(bf16[128,640]{1,0:T(8,128)(2,1)S(1)} %get-tuple-element.44), channel_id=1, source_target_pairs={{0,1},{1,0},{2,3},{3,2},{4,5},{5,4},{6,7},{7,6},{8,9},{9,8},{10,11... | collective-permute-start | bytes 491528 | tf_op jit(solution)/shard_map/ppermute | solution.py:364
  121.8 6.4 %collective-permute-start.9 = (bf16[128,640]{1,0:T(8,128)(2,1)S(1)}, bf16[128,640]{1,0:T(8,128)(2,1)S(1)}, u32[]{:S(2)}, u32[]{:S(2)}) collective-permute-start(bf16[128,640]{1,0:T(8,128)(2,1)S(1)} %get-tuple-element.45), channel_id=1, source_target_pairs={{0,5},{1,4},{2,7},{3,6},{4,1},{5,0},{6,3},{7,2},{8,13},{9,12},{10,... | collective-permute-start | bytes 491528 | tf_op jit(solution)/shard_map/ppermute | solution.py:364
  123.2 6.0 %collective-permute-start.8 = (bf16[128,640]{1,0:T(8,128)(2,1)S(1)}, bf16[128,640]{1,0:T(8,128)(2,1)S(1)}, u32[]{:S(2)}, u32[]{:S(2)}) collective-permute-start(bf16[128,640]{1,0:T(8,128)(2,1)S(1)} %get-tuple-element.46), channel_id=1, source_target_pairs={{0,4},{1,5},{2,6},{3,7},{4,0},{5,1},{6,2},{7,3},{8,12},{9,13},{10,... | collective-permute-start | bytes 491528 | tf_op jit(solution)/shard_map/ppermute | solution.py:364
  (14 other events, 11.8 us)
